TPU v7x, 32 devices: a whole 2x2x4 slice. The times are simulated.
32 devices in a mesh: gx: 16 (over z, y, core), gy: 2 (over x).
Axes of the slice: x: 2, y: 2, z: 4, core: 2. Of those that a mesh axis runs over, the one named last changes fastest.
Arguments:
- right_side: float32 [16, 2, 512, 256], P('gx', 'gy'), may hold values from -8 to 8, as said below
- coords: float32 [16, 2, 2, 512], P('gx', 'gy'), may hold values from 0 to 1
- noise: float32 [16, 2, 512], P('gx', 'gy'), may hold values from 0.25 to 1
- intersect: int32 [16, 2, 128], P('gx', 'gy'), may hold values from 0 to 4607, as said below
Outputs:
- solution: float32 [16, 2, 512, 256], P('gx', 'gy')
- residual: float32 [16, 2, 512, 256], P('gx', 'gy')
Inputs may be any that keep to these rules, and one draw needn't show every extreme that they name: `right_side`: right-hand sides of order one. `intersect`: each subdomain's list holds 128 distinct indices in increasing order; none names the subdomain itself (block number 4) or a subdomain beyond the first or last one along the second dimension.
All inputs are finite; a program needn't handle non-finite values.
Results may differ from a plain program's by a relative error of at most 0.0003.
Values sent between devices are 32-bit elements; how exact they have to be, the bound alone decides.
A program may use at most 128 MiB of HBM per device.

v0:
```python
import math
import jax
import jax.numpy as jnp
from jax import lax
from jax.sharding import PartitionSpec as P

ITERS = 3
RANGE_LEN = 0.25
ROOT_THREE = math.sqrt(3.0)
HIGH = lax.Precision.HIGHEST


def shifted(value, axis, by):
    count = lax.axis_size(axis)
    return lax.ppermute(value, axis, [(i, (i + by) % count) for i in range(count)])


def passed_along(block, axis, distance):
    devices = range(lax.axis_size(axis))
    route = [(i - distance, i) for i in devices if i - distance in devices]
    return lax.ppermute(block, axis, route)


def kernel_block(rows_pos, cols_pos):
    delta_x = rows_pos[0][:, None] - cols_pos[0][None, :]
    delta_y = rows_pos[1][:, None] - cols_pos[1][None, :]
    distance = jnp.sqrt(delta_x * delta_x + delta_y * delta_y)
    scaled = ROOT_THREE / RANGE_LEN * distance
    clipped = jnp.minimum(distance, 1.0)
    taper_val = jnp.square(jnp.square(1.0 - clipped)) * (4.0 * clipped + 1.0)
    return (1.0 + scaled) * jnp.exp(-scaled) * taper_val


def window_values(values):
    beside = {}
    for step_by in (1, -1):
        beside[step_by] = shifted(values, "gx", step_by)
    column = jnp.stack([beside[1], values, beside[-1]])
    across = {}
    for step_by in (1, -1):
        across[step_by] = passed_along(column, "gy", step_by)
    return [across[1], column, across[-1]]


def window_index(values):
    beside = {}
    for step_by in (1, -1):
        beside[step_by] = shifted(values, "gx", step_by)
    column = jnp.stack([beside[1], values, beside[-1]])
    across = {}
    for step_by in (1, -1):
        across[step_by] = passed_along(column, "gy", step_by)
    return [across[1], column, across[-1]]


def column_sum(first, second):
    return jnp.sum(first * second, axis=0)


def residual_dot(residue, precond):
    return lax.psum(column_sum(residue, precond), ("gx", "gy"))


def shards(right_side, coords, noise, intersect):
    points = right_side.shape[2]
    rhs_count = right_side.shape[3]
    intersect_len = intersect.shape[2]
    ext_len = points + intersect_len
    own_pos = coords.reshape(2, points)
    own_noise = noise.reshape(points)
    point_info = jnp.concatenate([own_pos, own_noise[None, :]], axis=0)
    info_cols = window_values(point_info)
    positions = [
        [
            jnp.stack(
                [
                    info_cols[col_off][row_off, 0] + float(row_off - 1),
                    info_cols[col_off][row_off, 1] + float(col_off - 1),
                ]
            )
            for col_off in range(3)
        ]
        for row_off in range(3)
    ]
    intersect_ids = intersect.reshape(intersect_len)
    block_id = intersect_ids // points
    row_in = intersect_ids % points
    row_of = block_id // 3
    col_of = block_id % 3
    local_id = row_of * points + row_in
    picked_info = [
        jnp.take(
            jnp.transpose(info_cols[col_off], (1, 0, 2)).reshape(3, 3 * points), local_id, axis=1
        )
        for col_off in range(3)
    ]
    chosen = jnp.where(
        col_of[None, :] == 0,
        picked_info[0],
        jnp.where(col_of[None, :] == 1, picked_info[1], picked_info[2]),
    )
    ov_pos = jnp.stack(
        [chosen[0] + (row_of - 1).astype(jnp.float32), chosen[1] + (col_of - 1).astype(jnp.float32)]
    )
    ext_pos = jnp.concatenate([own_pos, ov_pos], axis=1)
    ext_noise = jnp.concatenate([own_noise, chosen[2]])
    local_matrix = kernel_block(ext_pos, ext_pos) + jnp.diag(ext_noise)
    factor = jnp.linalg.cholesky(local_matrix)
    inv_factor = lax.linalg.triangular_solve(
        factor, jnp.eye(ext_len, dtype=jnp.float32), left_side=True, lower=True
    )
    inverse = jnp.dot(inv_factor.T, inv_factor, precision=HIGH, preferred_element_type=jnp.float32)
    near_ids = window_index(intersect_ids)
    point_iota = jnp.arange(points, dtype=jnp.int32)[:, None]
    row_base = (2 - jnp.arange(3, dtype=jnp.int32))[:, None] * 3
    selectors = []
    for col_off in range(3):
        own_rows = near_ids[col_off] - (row_base + (2 - col_off)) * points
        selectors.append((point_iota == own_rows.reshape(1, 3 * intersect_len)).astype(jnp.float32))

    def borrowed_rows(residue):
        requested = [
            lax.dot_general(
                selectors[col_off],
                residue,
                (((0,), (0,)), ((), ())),
                precision=HIGH,
                preferred_element_type=jnp.float32,
            ).reshape(3, intersect_len, rhs_count)
            for col_off in range(3)
        ]
        combined = jnp.stack([requested[col_off][1] for col_off in range(3)])
        for step_by, row_off in ((-1, 0), (1, 2)):
            outgoing = jnp.stack([requested[col_off][row_off] for col_off in range(3)])
            combined = combined + shifted(outgoing, "gx", step_by)
        gathered = combined[1]
        for step_by, col_off in ((-1, 0), (1, 2)):
            gathered = gathered + passed_along(combined[col_off], "gy", step_by)
        return gathered

    def precondition(residue):
        gathered = borrowed_rows(residue)
        extended = jnp.concatenate([residue, gathered], axis=0)
        solved = jnp.dot(inverse, extended, precision=HIGH, preferred_element_type=jnp.float32)
        returned = window_values(solved[points:])
        result = solved[:points]
        for col_off in range(3):
            result = result + jnp.dot(
                selectors[col_off],
                returned[col_off].reshape(3 * intersect_len, rhs_count),
                precision=HIGH,
                preferred_element_type=jnp.float32,
            )
        return result

    noise_col = own_noise[:, None]
    residual = right_side.reshape(points, rhs_count)
    solution = jnp.zeros_like(residual)
    precond = precondition(residual)
    direction = precond
    inner_now = residual_dot(residual, precond)
    for iteration in range(ITERS):
        columns = window_values(direction)
        accumulated = noise_col * direction
        for operate_row_off in range(3):
            for operate_col_off in range(3):
                accumulated = accumulated + jnp.dot(
                    kernel_block(own_pos, positions[operate_row_off][operate_col_off]),
                    columns[operate_col_off][operate_row_off],
                    precision=HIGH,
                    preferred_element_type=jnp.float32,
                )
        step_size = inner_now / lax.psum(column_sum(direction, accumulated), ("gx", "gy"))
        solution = solution + step_size * direction
        residual = residual - step_size * accumulated
        if iteration + 1 < ITERS:
            precond = precondition(residual)
            inner_next = residual_dot(residual, precond)
            direction = precond + inner_next / inner_now * direction
            inner_now = inner_next
    return (solution.reshape(1, 1, points, rhs_count), residual.reshape(1, 1, points, rhs_count))


def solution(mesh):
    placed = (
        P("gx", "gy", None, None),
        P("gx", "gy", None, None),
        P("gx", "gy", None),
        P("gx", "gy", None),
    )
    return jax.shard_map(
        shards,
        mesh=mesh,
        in_specs=placed,
        out_specs=(P("gx", "gy", None, None), P("gx", "gy", None, None)),
        check_vma=False,
    )
```

profile of v0, /device:TPU:0, one launch (start us, length us, event | category | flops | bytes accessed | tf_op | source)
XLA Modules:
  0.0 750.6 jit_solution(9324209336027450057)
XLA Ops:
  1.2 5.0 collective-permute-start.5
  7.0 4.4 collective-permute-start.1
  15.4 4.5 collective-permute-start.6
  23.5 3.7 collective-permute-start.2
  38.7 11.7 %cholesky.132 = f32[128,128]{1,0:T(8,128)S(1)} custom-call(f32[128,128]{1,0:T(8,128)S(1)} %cholesky.337), custom_call_target="Cholesky" | custom-call | tf_op jit(solution)/shard_map/jit(cholesky)/cholesky | solution.py:108
  50.6 9.8 %custom-call.38 = f32[1,128,128]{1,2,0:T(8,128)S(1)} custom-call(f32[1,128,128]{2,1,0:T(8,128)S(1)} %get-tuple-element.83), custom_call_target="InvertDiagBlocksLowerTriangular" | custom-call | tf_op jit(solution)/shard_map/jit(cholesky)/cholesky | solution.py:108
  63.0 11.9 %cholesky.270 = f32[128,128]{1,0:T(8,128)S(1)} custom-call(f32[128,128]{1,0:T(8,128)S(1)} %cholesky.341), custom_call_target="Cholesky" | custom-call | tf_op jit(solution)/shard_map/jit(cholesky)/cholesky | solution.py:108
  76.3 9.8 %custom-call.39 = f32[1,128,128]{1,2,0:T(8,128)S(1)} custom-call(f32[1,128,128]{2,1,0:T(8,128)S(1)} %get-tuple-element.80), custom_call_target="InvertDiagBlocksLowerTriangular" | custom-call | tf_op jit(solution)/shard_map/jit(cholesky)/cholesky | solution.py:108
  87.8 11.7 %cholesky.291 = f32[128,128]{1,0:T(8,128)S(1)} custom-call(f32[128,128]{1,0:T(8,128)S(1)} %cholesky.346), custom_call_target="Cholesky" | custom-call | tf_op jit(solution)/shard_map/jit(cholesky)/cholesky | solution.py:108
  100.3 9.8 %custom-call.40 = f32[1,128,128]{1,2,0:T(8,128)S(1)} custom-call(f32[1,128,128]{2,1,0:T(8,128)S(1)} %get-tuple-element.77), custom_call_target="InvertDiagBlocksLowerTriangular" | custom-call | tf_op jit(solution)/shard_map/jit(cholesky)/cholesky | solution.py:108
  112.0 11.7 %cholesky.310 = f32[128,128]{1,0:T(8,128)S(1)} custom-call(f32[128,128]{1,0:T(8,128)S(1)} %cholesky.351), custom_call_target="Cholesky" | custom-call | tf_op jit(solution)/shard_map/jit(cholesky)/cholesky | solution.py:108
  124.4 9.8 %custom-call.41 = f32[1,128,128]{1,2,0:T(8,128)S(1)} custom-call(f32[1,128,128]{2,1,0:T(8,128)S(1)} %get-tuple-element.74), custom_call_target="InvertDiagBlocksLowerTriangular" | custom-call | tf_op jit(solution)/shard_map/jit(cholesky)/cholesky | solution.py:108
  135.7 11.7 %cholesky.327 = f32[128,128]{1,0:T(8,128)S(1)} custom-call(f32[128,128]{1,0:T(8,128)S(1)} %convolution_subtract_fusion.6), custom_call_target="Cholesky" | custom-call | tf_op jit(solution)/shard_map/jit(cholesky)/cholesky | solution.py:108
  152.5 17.8 %while.1 = (s32[]{:T(128)}, f32[640,640]{1,0:T(8,128)}, s32[5,2]{0,1:T(2,128)S(1)}, f32[5,128,128]{2,1,0:T(8,128)}, s32[]{:T(128)}) while((s32[]{:T(128)}, f32[640,640]{1,0:T(8,128)}, s32[5,2]{0,1:T(2,128)S(1)}, f32[5,128,128]{2,1,0:T(8,128)}, s32[]{:T(128)}) %tuple.96), condition=%wide.while_cond, body=%wide.while_body.sunk | while | flops 2 | bytes 132705 | solution.py:109
  170.3 50.7 %custom-call.42 = f32[5,128,128]{1,2,0:T(8,128)} custom-call(f32[5,128,128]{2,1,0:T(8,128)} %get-tuple-element.10), custom_call_target="InvertDiagBlocksLowerTriangular" | custom-call | tf_op jit(solution)/shard_map/triangular_solve | solution.py:109
  234.1 4.7 collective-permute-start.11
  238.8 5.0 fusion.240
  245.7 4.4 collective-permute-start.13
  260.4 3.8 collective-permute-done.15
  264.9 4.4 collective-permute-start.17
  269.3 6.9 collective-permute-done.16
  285.3 26.6 %collective-permute-done.18 = f32[3,512,256]{2,1,0:T(8,128)S(1)} collective-permute-done((f32[3,512,256]{2,1,0:T(8,128)S(1)}, f32[3,512,256]{2,1,0:T(8,128)S(1)}, u32[]{:S(2)}, u32[]{:S(2)}) %collective-permute-start.18) | collective-permute-done | bytes 1572896 | tf_op jit(solution)/shard_map/ppermute | solution.py:21
  324.3 40.9 %all-reduce.1 = (f32[256]{0:T(256)S(1)}, f32[256]{0:T(256)S(1)}) all-reduce(f32[256]{0:T(256)S(1)} %get-tuple-element.12, f32[256]{0:T(256)S(1)} %get-tuple-element.11), channel_id=1, replica_groups=mesh['gx'=16,'gy'=2] {'gx','gy'}, use_global_device_ids=true, to_apply=%region_11.13 | all-reduce | flops 512 | bytes 4096 | tf_op jit(solution)/shard_map/psum | solution.py:61
  369.6 5.2 collective-permute-done.20
  374.7 4.8 collective-permute-done.21
  380.9 4.6 collective-permute-start.23
  391.3 4.1 collective-permute-start.25
  398.2 4.4 collective-permute-start.26
  404.5 7.1 collective-permute-done.26
  412.3 3.5 collective-permute-done.27
  417.2 36.8 %psum.44 = f32[256]{0:T(256)S(1)} all-reduce(f32[256]{0:T(256)S(1)} %get-tuple-element.128), channel_id=1, replica_groups=mesh['gx'=16,'gy'=2] {'gx','gy'}, use_global_device_ids=true, to_apply=%region_15.17 | all-reduce | flops 256 | bytes 2048 | tf_op jit(solution)/shard_map/psum | solution.py:61
  455.2 4.4 collective-permute-start.29
  459.6 7.0 collective-permute-done.28
  466.7 4.3 collective-permute-start.30
  478.3 24.6 %collective-permute-done.30 = f32[3,512,256]{2,1,0:T(8,128)S(1)} collective-permute-done((f32[3,512,256]{2,1,0:T(8,128)S(1)}, f32[3,512,256]{2,1,0:T(8,128)S(1)}, u32[]{:S(2)}, u32[]{:S(2)}) %collective-permute-start.30) | collective-permute-done | bytes 1572896 | tf_op jit(solution)/shard_map/ppermute | solution.py:21
  515.2 43.2 %psum.45 = f32[256]{0:T(256)S(1)} all-reduce(f32[256]{0:T(256)S(1)} %get-tuple-element.130), channel_id=1, replica_groups=mesh['gx'=16,'gy'=2] {'gx','gy'}, use_global_device_ids=true, to_apply=%region_17.19 | all-reduce | flops 256 | bytes 2048 | tf_op jit(solution)/shard_map/psum | solution.py:173
  562.8 5.2 collective-permute-done.32
  568.0 4.8 collective-permute-done.33
  574.2 4.6 collective-permute-start.35
  584.5 4.1 collective-permute-start.37
  591.4 4.4 collective-permute-start.38
  597.8 6.8 collective-permute-done.38
  609.4 36.9 %psum.46 = f32[256]{0:T(256)S(1)} all-reduce(f32[256]{0:T(256)S(1)} %get-tuple-element.132), channel_id=1, replica_groups=mesh['gx'=16,'gy'=2] {'gx','gy'}, use_global_device_ids=true, to_apply=%region_19.21 | all-reduce | flops 256 | bytes 2048 | tf_op jit(solution)/shard_map/psum | solution.py:61
  646.4 4.4 collective-permute-start.41
  650.8 7.0 collective-permute-done.40
  657.9 4.3 collective-permute-start.42
  669.3 25.0 %collective-permute-done.42 = f32[3,512,256]{2,1,0:T(8,128)S(1)} collective-permute-done((f32[3,512,256]{2,1,0:T(8,128)S(1)}, f32[3,512,256]{2,1,0:T(8,128)S(1)}, u32[]{:S(2)}, u32[]{:S(2)}) %collective-permute-start.42) | collective-permute-done | bytes 1572896 | tf_op jit(solution)/shard_map/ppermute | solution.py:21
  705.9 43.1 %psum.47 = f32[256]{0:T(256)S(1)} all-reduce(f32[256]{0:T(256)S(1)} %get-tuple-element.134), channel_id=1, replica_groups=mesh['gx'=16,'gy'=2] {'gx','gy'}, use_global_device_ids=true, to_apply=%region_21.23 | all-reduce | flops 256 | bytes 2048 | tf_op jit(solution)/shard_map/psum | solution.py:173
  (255 shorter events, 177.0 us)
Async XLA Ops:
  0.6 19.3 %copy-start = (f32[1,1,512,256]{3,2,1,0:T(8,128)S(1)}, f32[1,1,512,256]{3,2,1,0:T(8,128)}, u32[]{:S(2)}) copy-start(f32[1,1,512,256]{3,2,1,0:T(8,128)} %param.6) | copy-start | bytes 1572868
  0.7 13.4 %collective-permute-start.4 = (s32[128]{0:T(128)}, s32[128]{0:T(128)S(1)}, u32[]{:S(2)}, u32[]{:S(2)}) collective-permute-start(s32[128]{0:T(128)} %bitcast.373), channel_id=1, source_target_pairs={{0,2},{2,4},{4,6},{6,8},{8,10},{10,12},{12,14},{14,16},{16,18},{18... | collective-permute-start | bytes 1544 | tf_op jit(solution)/shard_map/ppermute | solution.py:15
  1.2 12.8 %collective-permute-start.5 = (s32[128]{0:T(128)}, s32[128]{0:T(128)S(1)}, u32[]{:S(2)}, u32[]{:S(2)}) collective-permute-start(s32[128]{0:T(128)} %bitcast.374), channel_id=1, source_target_pairs={{0,30},{2,0},{4,2},{6,4},{8,6},{10,8},{12,10},{14,12},{16,14},{18,... | collective-permute-start | bytes 1544 | tf_op jit(solution)/shard_map/ppermute | solution.py:15
  7.0 16.5 %collective-permute-start = (f32[3,512]{1,0:T(4,128)S(1)}, f32[3,512]{1,0:T(4,128)S(1)}, u32[]{:S(2)}, u32[]{:S(2)}) collective-permute-start(f32[3,512]{1,0:T(4,128)S(1)} %get-tuple-element.110), channel_id=1, source_target_pairs={{0,2},{2,4},{4,6},{6,8},{8,10},{10,12},{12,14},{14,16},{16,18},{18... | collective-permute-start | bytes 18440 | tf_op jit(solution)/shard_map/ppermute | solution.py:15
  7.0 16.4 %collective-permute-start.1 = (f32[3,512]{1,0:T(4,128)S(1)}, f32[3,512]{1,0:T(4,128)S(1)}, u32[]{:S(2)}, u32[]{:S(2)}) collective-permute-start(f32[3,512]{1,0:T(4,128)S(1)} %get-tuple-element.110), channel_id=1, source_target_pairs={{0,30},{2,0},{4,2},{6,4},{8,6},{10,8},{12,10},{14,12},{16,14},{18,... | collective-permute-start | bytes 18440 | tf_op jit(solution)/shard_map/ppermute | solution.py:15
  14.1 6.7 collective-permute-start.7
  15.4 6.3 collective-permute-start.6
  23.5 208.1 %collective-permute-start.8 = (f32[3,128,256]{2,1,0:T(8,128)}, f32[3,128,256]{2,1,0:T(8,128)}, u32[]{:S(2)}, u32[]{:S(2)}) collective-permute-start(f32[3,128,256]{2,1,0:T(8,128)} %pad_maximum_fusion.3), channel_id=1, source_target_pairs={{0,30},{2,0},{4,2},{6,4},{8,6},{10,8},{12,10},{14,12},{16,14},{18,... | collective-permute-start | bytes 1179656 | tf_op jit(solution)/shard_map/ppermute | solution.py:15
  23.5 7.5 collective-permute-start.2
  27.2 5.7 collective-permute-start.3
  29.3 202.3 %collective-permute-start.9 = (f32[3,128,256]{2,1,0:T(8,128)}, f32[3,128,256]{2,1,0:T(8,128)}, u32[]{:S(2)}, u32[]{:S(2)}) collective-permute-start(f32[3,128,256]{2,1,0:T(8,128)} %pad_maximum_fusion.4), channel_id=1, source_target_pairs={{0,2},{2,4},{4,6},{6,8},{8,10},{10,12},{12,14},{14,16},{16,18},{18... | collective-permute-start | bytes 1179656 | tf_op jit(solution)/shard_map/ppermute | solution.py:15
  170.3 54.7 %copy-start.3 = (f32[640,640]{1,0:T(8,128)S(1)}, f32[640,640]{1,0:T(8,128)}, u32[]{:S(2)}) copy-start(f32[640,640]{1,0:T(8,128)} %fusion.25) | copy-start | bytes 4915204
  232.8 11.1 %collective-permute-start.10 = (f32[128,256]{1,0:T(8,128)S(1)}, f32[128,256]{1,0:T(8,128)S(1)}, u32[]{:S(2)}, u32[]{:S(2)}) collective-permute-start(f32[128,256]{1,0:T(8,128)S(1)} %get-tuple-element.60), channel_id=1, source_target_pairs={{1,0},{3,2},{5,4},{7,6},{9,8},{11,10},{13,12},{15,14},{17,16},{19,... | collective-permute-start | bytes 393224 | tf_op jit(solution)/shard_map/ppermute | solution.py:21
  234.1 9.8 %collective-permute-start.11 = (f32[128,256]{1,0:T(8,128)S(1)}, f32[128,256]{1,0:T(8,128)S(1)}, u32[]{:S(2)}, u32[]{:S(2)}) collective-permute-start(f32[128,256]{1,0:T(8,128)S(1)} %get-tuple-element.61), channel_id=1, source_target_pairs={{0,1},{2,3},{4,5},{6,7},{8,9},{10,11},{12,13},{14,15},{16,17},{18,... | collective-permute-start | bytes 393224 | tf_op jit(solution)/shard_map/ppermute | solution.py:21
  245.7 7.1 collective-permute-start.12
  245.7 7.1 collective-permute-start.13
  252.9 6.9 collective-permute-start.14
  254.5 9.7 %collective-permute-start.15 = (f32[3,128,256]{2,1,0:T(8,128)S(1)}, f32[3,128,256]{2,1,0:T(8,128)S(1)}, u32[]{:S(2)}, u32[]{:S(2)}) collective-permute-start(f32[3,128,256]{2,1,0:T(8,128)S(1)} %pad_maximum_fusion.5), channel_id=1, source_target_pairs={{1,0},{3,2},{5,4},{7,6},{9,8},{11,10},{13,12},{15,14},{17,16},{19,... | collective-permute-start | bytes 1179656 | tf_op jit(solution)/shard_map/ppermute | solution.py:21
  264.8 11.5 %collective-permute-start.16 = (f32[512,256]{1,0:T(8,128)S(1)}, f32[512,256]{1,0:T(8,128)S(1)}, u32[]{:S(2)}, u32[]{:S(2)}) collective-permute-start(f32[512,256]{1,0:T(8,128)S(1)} %convolution_add_fusion.5), channel_id=1, source_target_pairs={{0,2},{2,4},{4,6},{6,8},{8,10},{10,12},{12,14},{14,16},{16,18},{18... | collective-permute-start | bytes 1572872 | tf_op jit(solution)/shard_map/ppermute | solution.py:15
  264.9 11.4 %collective-permute-start.17 = (f32[512,256]{1,0:T(8,128)S(1)}, f32[512,256]{1,0:T(8,128)S(1)}, u32[]{:S(2)}, u32[]{:S(2)}) collective-permute-start(f32[512,256]{1,0:T(8,128)S(1)} %convolution_add_fusion.5), channel_id=1, source_target_pairs={{0,30},{2,0},{4,2},{6,4},{8,6},{10,8},{12,10},{14,12},{16,14},{18,... | collective-permute-start | bytes 1572872 | tf_op jit(solution)/shard_map/ppermute | solution.py:15
  276.4 35.5 %collective-permute-start.18 = (f32[3,512,256]{2,1,0:T(8,128)S(1)}, f32[3,512,256]{2,1,0:T(8,128)S(1)}, u32[]{:S(2)}, u32[]{:S(2)}) collective-permute-start(f32[3,512,256]{2,1,0:T(8,128)S(1)} %pad_maximum_fusion), channel_id=1, source_target_pairs={{0,1},{2,3},{4,5},{6,7},{8,9},{10,11},{12,13},{14,15},{16,17},{18,... | collective-permute-start | bytes 4718600 | tf_op jit(solution)/shard_map/ppermute | solution.py:21
  278.0 39.5 %collective-permute-start.19 = (f32[3,512,256]{2,1,0:T(8,128)S(1)}, f32[3,512,256]{2,1,0:T(8,128)S(1)}, u32[]{:S(2)}, u32[]{:S(2)}) collective-permute-start(f32[3,512,256]{2,1,0:T(8,128)S(1)} %pad_maximum_fusion), channel_id=1, source_target_pairs={{1,0},{3,2},{5,4},{7,6},{9,8},{11,10},{13,12},{15,14},{17,16},{19,... | collective-permute-start | bytes 4718600 | tf_op jit(solution)/shard_map/ppermute | solution.py:21
  368.9 5.8 collective-permute-start.20
  369.5 10.1 %collective-permute-start.21 = (f32[3,128,256]{2,1,0:T(8,128)S(1)}, f32[3,128,256]{2,1,0:T(8,128)S(1)}, u32[]{:S(2)}, u32[]{:S(2)}) collective-permute-start(f32[3,128,256]{2,1,0:T(8,128)S(1)} %pad_maximum_fusion.7), channel_id=1, source_target_pairs={{0,2},{2,4},{4,6},{6,8},{8,10},{10,12},{12,14},{14,16},{16,18},{18... | collective-permute-start | bytes 1179656 | tf_op jit(solution)/shard_map/ppermute | solution.py:15
  379.6 7.7 %collective-permute-start.22 = (f32[128,256]{1,0:T(8,128)S(1)}, f32[128,256]{1,0:T(8,128)S(1)}, u32[]{:S(2)}, u32[]{:S(2)}) collective-permute-start(f32[128,256]{1,0:T(8,128)S(1)} %get-tuple-element.49), channel_id=1, source_target_pairs={{1,0},{3,2},{5,4},{7,6},{9,8},{11,10},{13,12},{15,14},{17,16},{19,... | collective-permute-start | bytes 393224 | tf_op jit(solution)/shard_map/ppermute | solution.py:21
  380.9 8.2 %collective-permute-start.23 = (f32[128,256]{1,0:T(8,128)S(1)}, f32[128,256]{1,0:T(8,128)S(1)}, u32[]{:S(2)}, u32[]{:S(2)}) collective-permute-start(f32[128,256]{1,0:T(8,128)S(1)} %get-tuple-element.50), channel_id=1, source_target_pairs={{0,1},{2,3},{4,5},{6,7},{8,9},{10,11},{12,13},{14,15},{16,17},{18,... | collective-permute-start | bytes 393224 | tf_op jit(solution)/shard_map/ppermute | solution.py:21
  390.9 7.2 collective-permute-start.24
  391.3 6.8 collective-permute-start.25
  398.2 13.5 %collective-permute-start.26 = (f32[3,128,256]{2,1,0:T(8,128)S(1)}, f32[3,128,256]{2,1,0:T(8,128)S(1)}, u32[]{:S(2)}, u32[]{:S(2)}) collective-permute-start(f32[3,128,256]{2,1,0:T(8,128)S(1)} %pad_maximum_fusion.8), channel_id=1, source_target_pairs={{0,1},{2,3},{4,5},{6,7},{8,9},{10,11},{12,13},{14,15},{16,17},{18,... | collective-permute-start | bytes 1179656 | tf_op jit(solution)/shard_map/ppermute | solution.py:21
  402.6 13.2 %collective-permute-start.27 = (f32[3,128,256]{2,1,0:T(8,128)S(1)}, f32[3,128,256]{2,1,0:T(8,128)S(1)}, u32[]{:S(2)}, u32[]{:S(2)}) collective-permute-start(f32[3,128,256]{2,1,0:T(8,128)S(1)} %pad_maximum_fusion.8), channel_id=1, source_target_pairs={{1,0},{3,2},{5,4},{7,6},{9,8},{11,10},{13,12},{15,14},{17,16},{19,... | collective-permute-start | bytes 1179656 | tf_op jit(solution)/shard_map/ppermute | solution.py:21
  455.1 57.2 %copy-start.1 = (f32[512,256]{1,0:T(8,128)}, f32[512,256]{1,0:T(8,128)S(1)}, u32[]{:S(2)}) copy-start(f32[512,256]{1,0:T(8,128)S(1)} %multiply_add_fusion.1) | copy-start | bytes 1572868
  455.1 11.5 %collective-permute-start.28 = (f32[512,256]{1,0:T(8,128)S(1)}, f32[512,256]{1,0:T(8,128)S(1)}, u32[]{:S(2)}, u32[]{:S(2)}) collective-permute-start(f32[512,256]{1,0:T(8,128)S(1)} %multiply_add_fusion.1), channel_id=1, source_target_pairs={{0,2},{2,4},{4,6},{6,8},{8,10},{10,12},{12,14},{14,16},{16,18},{18... | collective-permute-start | bytes 1572872 | tf_op jit(solution)/shard_map/ppermute | solution.py:15
  455.2 11.4 %collective-permute-start.29 = (f32[512,256]{1,0:T(8,128)S(1)}, f32[512,256]{1,0:T(8,128)S(1)}, u32[]{:S(2)}, u32[]{:S(2)}) collective-permute-start(f32[512,256]{1,0:T(8,128)S(1)} %multiply_add_fusion.1), channel_id=1, source_target_pairs={{0,30},{2,0},{4,2},{6,4},{8,6},{10,8},{12,10},{14,12},{16,14},{18,... | collective-permute-start | bytes 1572872 | tf_op jit(solution)/shard_map/ppermute | solution.py:15
  466.7 36.1 %collective-permute-start.30 = (f32[3,512,256]{2,1,0:T(8,128)S(1)}, f32[3,512,256]{2,1,0:T(8,128)S(1)}, u32[]{:S(2)}, u32[]{:S(2)}) collective-permute-start(f32[3,512,256]{2,1,0:T(8,128)S(1)} %pad_maximum_fusion.1), channel_id=1, source_target_pairs={{0,1},{2,3},{4,5},{6,7},{8,9},{10,11},{12,13},{14,15},{16,17},{18,... | collective-permute-start | bytes 4718600 | tf_op jit(solution)/shard_map/ppermute | solution.py:21
  471.0 37.4 %collective-permute-start.31 = (f32[3,512,256]{2,1,0:T(8,128)S(1)}, f32[3,512,256]{2,1,0:T(8,128)S(1)}, u32[]{:S(2)}, u32[]{:S(2)}) collective-permute-start(f32[3,512,256]{2,1,0:T(8,128)S(1)} %pad_maximum_fusion.1), channel_id=1, source_target_pairs={{1,0},{3,2},{5,4},{7,6},{9,8},{11,10},{13,12},{15,14},{17,16},{19,... | collective-permute-start | bytes 4718600 | tf_op jit(solution)/shard_map/ppermute | solution.py:21
  562.1 5.9 collective-permute-start.32
  562.7 10.1 %collective-permute-start.33 = (f32[3,128,256]{2,1,0:T(8,128)S(1)}, f32[3,128,256]{2,1,0:T(8,128)S(1)}, u32[]{:S(2)}, u32[]{:S(2)}) collective-permute-start(f32[3,128,256]{2,1,0:T(8,128)S(1)} %pad_maximum_fusion.10), channel_id=1, source_target_pairs={{0,2},{2,4},{4,6},{6,8},{8,10},{10,12},{12,14},{14,16},{16,18},{18... | collective-permute-start | bytes 1179656 | tf_op jit(solution)/shard_map/ppermute | solution.py:15
  572.9 7.8 %collective-permute-start.34 = (f32[128,256]{1,0:T(8,128)S(1)}, f32[128,256]{1,0:T(8,128)S(1)}, u32[]{:S(2)}, u32[]{:S(2)}) collective-permute-start(f32[128,256]{1,0:T(8,128)S(1)} %get-tuple-element.38), channel_id=1, source_target_pairs={{1,0},{3,2},{5,4},{7,6},{9,8},{11,10},{13,12},{15,14},{17,16},{19,... | collective-permute-start | bytes 393224 | tf_op jit(solution)/shard_map/ppermute | solution.py:21
  574.2 8.2 %collective-permute-start.35 = (f32[128,256]{1,0:T(8,128)S(1)}, f32[128,256]{1,0:T(8,128)S(1)}, u32[]{:S(2)}, u32[]{:S(2)}) collective-permute-start(f32[128,256]{1,0:T(8,128)S(1)} %get-tuple-element.39), channel_id=1, source_target_pairs={{0,1},{2,3},{4,5},{6,7},{8,9},{10,11},{12,13},{14,15},{16,17},{18,... | collective-permute-start | bytes 393224 | tf_op jit(solution)/shard_map/ppermute | solution.py:21
  584.2 7.2 collective-permute-start.36
  584.5 6.9 collective-permute-start.37
  591.4 13.1 %collective-permute-start.38 = (f32[3,128,256]{2,1,0:T(8,128)S(1)}, f32[3,128,256]{2,1,0:T(8,128)S(1)}, u32[]{:S(2)}, u32[]{:S(2)}) collective-permute-start(f32[3,128,256]{2,1,0:T(8,128)S(1)} %pad_maximum_fusion.11), channel_id=1, source_target_pairs={{0,1},{2,3},{4,5},{6,7},{8,9},{10,11},{12,13},{14,15},{16,17},{18,... | collective-permute-start | bytes 1179656 | tf_op jit(solution)/shard_map/ppermute | solution.py:21
  595.9 12.8 %collective-permute-start.39 = (f32[3,128,256]{2,1,0:T(8,128)S(1)}, f32[3,128,256]{2,1,0:T(8,128)S(1)}, u32[]{:S(2)}, u32[]{:S(2)}) collective-permute-start(f32[3,128,256]{2,1,0:T(8,128)S(1)} %pad_maximum_fusion.11), channel_id=1, source_target_pairs={{1,0},{3,2},{5,4},{7,6},{9,8},{11,10},{13,12},{15,14},{17,16},{19,... | collective-permute-start | bytes 1179656 | tf_op jit(solution)/shard_map/ppermute | solution.py:21
  605.2 41.1 %copy-start.2 = (f32[512,256]{1,0:T(8,128)S(1)}, f32[512,256]{1,0:T(8,128)}, u32[]{:S(2)}) copy-start(f32[512,256]{1,0:T(8,128)} %copy-done.1) | copy-start | bytes 1572868
  646.3 11.5 %collective-permute-start.40 = (f32[512,256]{1,0:T(8,128)S(1)}, f32[512,256]{1,0:T(8,128)S(1)}, u32[]{:S(2)}, u32[]{:S(2)}) collective-permute-start(f32[512,256]{1,0:T(8,128)S(1)} %multiply_add_fusion), channel_id=1, source_target_pairs={{0,2},{2,4},{4,6},{6,8},{8,10},{10,12},{12,14},{14,16},{16,18},{18... | collective-permute-start | bytes 1572872 | tf_op jit(solution)/shard_map/ppermute | solution.py:15
  646.4 11.4 %collective-permute-start.41 = (f32[512,256]{1,0:T(8,128)S(1)}, f32[512,256]{1,0:T(8,128)S(1)}, u32[]{:S(2)}, u32[]{:S(2)}) collective-permute-start(f32[512,256]{1,0:T(8,128)S(1)} %multiply_add_fusion), channel_id=1, source_target_pairs={{0,30},{2,0},{4,2},{6,4},{8,6},{10,8},{12,10},{14,12},{16,14},{18,... | collective-permute-start | bytes 1572872 | tf_op jit(solution)/shard_map/ppermute | solution.py:15
  657.9 36.3 %collective-permute-start.42 = (f32[3,512,256]{2,1,0:T(8,128)S(1)}, f32[3,512,256]{2,1,0:T(8,128)S(1)}, u32[]{:S(2)}, u32[]{:S(2)}) collective-permute-start(f32[3,512,256]{2,1,0:T(8,128)S(1)} %pad_maximum_fusion.2), channel_id=1, source_target_pairs={{0,1},{2,3},{4,5},{6,7},{8,9},{10,11},{12,13},{14,15},{16,17},{18,... | collective-permute-start | bytes 4718600 | tf_op jit(solution)/shard_map/ppermute | solution.py:21
  662.2 37.6 %collective-permute-start.43 = (f32[3,512,256]{2,1,0:T(8,128)S(1)}, f32[3,512,256]{2,1,0:T(8,128)S(1)}, u32[]{:S(2)}, u32[]{:S(2)}) collective-permute-start(f32[3,512,256]{2,1,0:T(8,128)S(1)} %pad_maximum_fusion.2), channel_id=1, source_target_pairs={{1,0},{3,2},{5,4},{7,6},{9,8},{11,10},{13,12},{15,14},{17,16},{19,... | collective-permute-start | bytes 4718600 | tf_op jit(solution)/shard_map/ppermute | solution.py:21
  (5 other events, 28.6 us)
where the time goes:
time: 756 us; the launch traced here: 751 us
  blocking collectives  201 us (27%)
  other arithmetic  168 us (22%)
  waiting for transfers between devices  161 us (21%)
  starting transfers between devices  96.9 us (13%)
  matrix products  94.8 us (13%)
  local copies, waits for them, and re-layouts  22.5 us (3%)
    psum x3, blocking collectives, residual_dot(): return lax.psum(column_sum(residue, precond), ('gx', 'gy'))  115 us
    ppermute x22, waiting for transfers between devices, passed_along(): return lax.ppermute(block, axis, route)  112 us
    another operation x19, other arithmetic, shards(): factor = jnp.linalg.cholesky(local_matrix)  101 us
    psum x2, blocking collectives, shards(): lax.psum(column_sum(direction, accumulated), ('gx', 'gy'))  86.3 us
    ppermute x22, starting transfers between devices, passed_along(): return lax.ppermute(block, axis, route)  57.9 us
    dot_general x27, matrix products, shards(): jnp.dot(kernel_block(own_pos, positions[operate_row_off][operate_col_off]...  52.9 us
    another operation x3, other arithmetic, shards(): lax.linalg.triangular_solve(factor, jnp.eye(ext_len, dtype=jnp.float32),...  52 us
    ppermute x22, waiting for transfers between devices, shifted(): lax.ppermute(value, axis, [(i, (i + by) % count) for i in range(count)])  49 us
  transfers between devices with their start and end apart: 44, of which 24 were waited for; matrix products, arithmetic and copies ran while one was open for 33% of the time, Pallas kernels for 0%

commit v1 on v0

--- a/solution.py
+++ b/solution.py
@@ -8,6 +8,11 @@
 RANGE_LEN = 0.25
 ROOT_THREE = math.sqrt(3.0)
 HIGH = lax.Precision.HIGHEST
+
+
+def start_the_modes(obj):
+    small = jnp.sum(lax.all_gather(obj, axis_name=("gx", "gy")), axis=0)
+    return small
 
 
 def shifted(value, axis, by):
@@ -58,7 +63,7 @@
 
 
 def residual_dot(residue, precond):
-    return lax.psum(column_sum(residue, precond), ("gx", "gy"))
+    return start_the_modes(column_sum(residue, precond))
 
 
 def shards(right_side, coords, noise, intersect):

time: 756 us -> 864 us (1.14)
  blocking collectives: 201 us -> 309 us
    all_gather x0 -> x3, blocking collectives: none -> 198 us  [start_the_modes(): small = jnp.sum(lax.all_gather(obj, axis_name=('gx', 'gy')), axis=0)]
    psum x3 -> x0, blocking collectives: 115 us -> none  [residual_dot(): return lax.psum(column_sum(residue, precond), ('gx', 'gy'))]
    psum x2 -> x3, blocking collectives: 86.3 us -> 111 us  [shards(): lax.psum(column_sum(direction, accumulated), ('gx', 'gy'))]
  transfers between devices with their start and end apart: 44 -> 44, of which waited for: 24 -> 24; matrix products, arithmetic and copies ran while one was open for 33% -> 29% of each run, Pallas kernels for 0% -> 0%
where the time goes in v1:
time: 864 us; the launch traced here: 858 us
  blocking collectives  309 us (36%)
  other arithmetic  168 us (19%)
  waiting for transfers between devices  158 us (18%)
  starting transfers between devices  98.1 us (11%)
  matrix products  94.8 us (11%)
  local copies, waits for them, and re-layouts  23 us (3%)
    all_gather x3, blocking collectives, start_the_modes(): small = jnp.sum(lax.all_gather(obj, axis_name=('gx', 'gy')), axis=0)  198 us
    psum x3, blocking collectives, shards(): lax.psum(column_sum(direction, accumulated), ('gx', 'gy'))  111 us
    ppermute x22, waiting for transfers between devices, passed_along(): return lax.ppermute(block, axis, route)  109 us
    another operation x19, other arithmetic, shards(): factor = jnp.linalg.cholesky(local_matrix)  102 us
    ppermute x22, starting transfers between devices, passed_along(): return lax.ppermute(block, axis, route)  55.8 us
    dot_general x27, matrix products, shards(): jnp.dot(kernel_block(own_pos, positions[operate_row_off][operate_col_off]...  52.9 us
    another operation x3, other arithmetic, shards(): lax.linalg.triangular_solve(factor, jnp.eye(ext_len, dtype=jnp.float32),...  52 us
    ppermute x22, waiting for transfers between devices, shifted(): lax.ppermute(value, axis, [(i, (i + by) % count) for i in range(count)])  48.8 us
  transfers between devices with their start and end apart: 44, of which 24 were waited for; matrix products, arithmetic and copies ran while one was open for 29% of the time, Pallas kernels for 0%

profile of v1, /device:TPU:0, one launch (start us, length us, event | category | flops | bytes accessed | tf_op | source)
XLA Modules:
  0.0 857.5 jit_solution(15242717837358744038)
XLA Ops:
  1.2 5.0 collective-permute-start.5
  7.0 4.4 collective-permute-start.1
  15.4 4.5 collective-permute-start.6
  23.5 3.7 collective-permute-start.2
  38.7 11.7 %cholesky.132 = f32[128,128]{1,0:T(8,128)S(1)} custom-call(f32[128,128]{1,0:T(8,128)S(1)} %cholesky.337), custom_call_target="Cholesky" | custom-call | tf_op jit(solution)/shard_map/jit(cholesky)/cholesky | solution.py:113
  50.6 9.8 %custom-call.38 = f32[1,128,128]{1,2,0:T(8,128)S(1)} custom-call(f32[1,128,128]{2,1,0:T(8,128)S(1)} %get-tuple-element.81), custom_call_target="InvertDiagBlocksLowerTriangular" | custom-call | tf_op jit(solution)/shard_map/jit(cholesky)/cholesky | solution.py:113
  63.0 11.9 %cholesky.270 = f32[128,128]{1,0:T(8,128)S(1)} custom-call(f32[128,128]{1,0:T(8,128)S(1)} %cholesky.341), custom_call_target="Cholesky" | custom-call | tf_op jit(solution)/shard_map/jit(cholesky)/cholesky | solution.py:113
  76.3 9.8 %custom-call.39 = f32[1,128,128]{1,2,0:T(8,128)S(1)} custom-call(f32[1,128,128]{2,1,0:T(8,128)S(1)} %get-tuple-element.78), custom_call_target="InvertDiagBlocksLowerTriangular" | custom-call | tf_op jit(solution)/shard_map/jit(cholesky)/cholesky | solution.py:113
  87.9 11.7 %cholesky.291 = f32[128,128]{1,0:T(8,128)S(1)} custom-call(f32[128,128]{1,0:T(8,128)S(1)} %cholesky.346), custom_call_target="Cholesky" | custom-call | tf_op jit(solution)/shard_map/jit(cholesky)/cholesky | solution.py:113
  100.4 9.8 %custom-call.40 = f32[1,128,128]{1,2,0:T(8,128)S(1)} custom-call(f32[1,128,128]{2,1,0:T(8,128)S(1)} %get-tuple-element.75), custom_call_target="InvertDiagBlocksLowerTriangular" | custom-call | tf_op jit(solution)/shard_map/jit(cholesky)/cholesky | solution.py:113
  112.1 11.7 %cholesky.310 = f32[128,128]{1,0:T(8,128)S(1)} custom-call(f32[128,128]{1,0:T(8,128)S(1)} %cholesky.351), custom_call_target="Cholesky" | custom-call | tf_op jit(solution)/shard_map/jit(cholesky)/cholesky | solution.py:113
  124.4 9.8 %custom-call.41 = f32[1,128,128]{1,2,0:T(8,128)S(1)} custom-call(f32[1,128,128]{2,1,0:T(8,128)S(1)} %get-tuple-element.72), custom_call_target="InvertDiagBlocksLowerTriangular" | custom-call | tf_op jit(solution)/shard_map/jit(cholesky)/cholesky | solution.py:113
  135.7 11.7 %cholesky.327 = f32[128,128]{1,0:T(8,128)S(1)} custom-call(f32[128,128]{1,0:T(8,128)S(1)} %convolution_subtract_fusion.6), custom_call_target="Cholesky" | custom-call | tf_op jit(solution)/shard_map/jit(cholesky)/cholesky | solution.py:113
  152.7 18.3 %while.1 = (s32[]{:T(128)}, f32[640,640]{1,0:T(8,128)}, s32[5,2]{0,1:T(2,128)S(1)}, f32[5,128,128]{2,1,0:T(8,128)}, s32[]{:T(128)}) while((s32[]{:T(128)}, f32[640,640]{1,0:T(8,128)}, s32[5,2]{0,1:T(2,128)S(1)}, f32[5,128,128]{2,1,0:T(8,128)}, s32[]{:T(128)}) %tuple.96), condition=%wide.while_cond, body=%wide.while_body.sunk | while | flops 2 | bytes 132705 | solution.py:114
  171.0 50.7 %custom-call.42 = f32[5,128,128]{1,2,0:T(8,128)} custom-call(f32[5,128,128]{2,1,0:T(8,128)} %get-tuple-element.10), custom_call_target="InvertDiagBlocksLowerTriangular" | custom-call | tf_op jit(solution)/shard_map/triangular_solve | solution.py:114
  234.8 4.7 collective-permute-start.11
  239.5 5.0 fusion.240
  246.4 4.4 collective-permute-start.13
  261.0 3.8 collective-permute-done.15
  265.5 4.4 collective-permute-start.17
  270.0 6.9 collective-permute-done.16
  286.0 26.6 %collective-permute-done.18 = f32[3,512,256]{2,1,0:T(8,128)S(1)} collective-permute-done((f32[3,512,256]{2,1,0:T(8,128)S(1)}, f32[3,512,256]{2,1,0:T(8,128)S(1)}, u32[]{:S(2)}, u32[]{:S(2)}) %collective-permute-start.18) | collective-permute-done | bytes 1572896 | tf_op jit(solution)/shard_map/ppermute | solution.py:26
  324.9 68.8 %all-gather.3 = f32[32,1,256]{2,1,0:T(1,128)S(1)} all-gather(f32[1,1,256]{2,1,0:T(1,128)S(1)} %bitcast.495), channel_id=2, replica_groups=mesh['gx'=16,'gy'=2] {'gx','gy'}, dimensions={0}, use_global_device_ids=true | all-gather | bytes 33792 | tf_op jit(solution)/shard_map/all_gather | solution.py:14
  393.8 36.8 %psum.21 = f32[256]{0:T(256)S(1)} all-reduce(f32[256]{0:T(256)S(1)} %get-tuple-element.11), channel_id=1, replica_groups=mesh['gx'=16,'gy'=2] {'gx','gy'}, use_global_device_ids=true, to_apply=%region_13.15 | all-reduce | flops 256 | bytes 2048 | tf_op jit(solution)/shard_map/psum | solution.py:178
  435.7 5.2 collective-permute-done.20
  440.9 4.8 collective-permute-done.21
  447.1 4.6 collective-permute-start.23
  456.9 4.4 collective-permute-start.25
  464.1 4.4 collective-permute-start.26
  470.5 6.9 collective-permute-done.26
  477.9 3.5 collective-permute-done.27
  482.9 63.6 %all-gather.4 = f32[32,1,256]{2,1,0:T(1,128)S(1)} all-gather(f32[1,1,256]{2,1,0:T(1,128)S(1)} %bitcast.386), channel_id=3, replica_groups=mesh['gx'=16,'gy'=2] {'gx','gy'}, dimensions={0}, use_global_device_ids=true | all-gather | bytes 33792 | tf_op jit(solution)/shard_map/all_gather | solution.py:14
  547.7 4.4 collective-permute-start.29
  552.1 7.0 collective-permute-done.28
  559.2 4.1 collective-permute-start.30
  570.6 24.3 %collective-permute-done.30 = f32[3,512,256]{2,1,0:T(8,128)S(1)} collective-permute-done((f32[3,512,256]{2,1,0:T(8,128)S(1)}, f32[3,512,256]{2,1,0:T(8,128)S(1)}, u32[]{:S(2)}, u32[]{:S(2)}) %collective-permute-start.30) | collective-permute-done | bytes 1572896 | tf_op jit(solution)/shard_map/ppermute | solution.py:26
  607.2 37.3 %psum.22 = f32[256]{0:T(256)S(1)} all-reduce(f32[256]{0:T(256)S(1)} %get-tuple-element.128), channel_id=1, replica_groups=mesh['gx'=16,'gy'=2] {'gx','gy'}, use_global_device_ids=true, to_apply=%region_17.19 | all-reduce | flops 256 | bytes 2048 | tf_op jit(solution)/shard_map/psum | solution.py:178
  651.5 5.2 collective-permute-done.32
  656.7 4.7 collective-permute-done.33
  662.8 4.6 collective-permute-start.35
  671.7 4.4 collective-permute-start.37
  678.8 4.4 collective-permute-start.38
  685.1 4.7 collective-permute-done.38
  694.6 65.2 %all-gather.5 = f32[32,1,256]{2,1,0:T(1,128)S(1)} all-gather(f32[1,1,256]{2,1,0:T(1,128)S(1)} %bitcast.385), channel_id=4, replica_groups=mesh['gx'=16,'gy'=2] {'gx','gy'}, dimensions={0}, use_global_device_ids=true | all-gather | bytes 33792 | tf_op jit(solution)/shard_map/all_gather | solution.py:14
  760.1 4.4 collective-permute-start.41
  764.5 7.0 collective-permute-done.40
  781.1 25.9 %collective-permute-done.42 = f32[3,512,256]{2,1,0:T(8,128)S(1)} collective-permute-done((f32[3,512,256]{2,1,0:T(8,128)S(1)}, f32[3,512,256]{2,1,0:T(8,128)S(1)}, u32[]{:S(2)}, u32[]{:S(2)}) %collective-permute-start.42) | collective-permute-done | bytes 1572896 | tf_op jit(solution)/shard_map/ppermute | solution.py:26
  818.6 37.3 %psum.23 = f32[256]{0:T(256)S(1)} all-reduce(f32[256]{0:T(256)S(1)} %get-tuple-element.132), channel_id=1, replica_groups=mesh['gx'=16,'gy'=2] {'gx','gy'}, use_global_device_ids=true, to_apply=%region_21.23 | all-reduce | flops 256 | bytes 2048 | tf_op jit(solution)/shard_map/psum | solution.py:178
  (259 shorter events, 181.3 us)
Async XLA Ops:
  0.6 19.3 %copy-start = (f32[1,1,512,256]{3,2,1,0:T(8,128)S(1)}, f32[1,1,512,256]{3,2,1,0:T(8,128)}, u32[]{:S(2)}) copy-start(f32[1,1,512,256]{3,2,1,0:T(8,128)} %param.6) | copy-start | bytes 1572868
  0.7 13.4 %collective-permute-start.4 = (s32[128]{0:T(128)}, s32[128]{0:T(128)S(1)}, u32[]{:S(2)}, u32[]{:S(2)}) collective-permute-start(s32[128]{0:T(128)} %bitcast.376), channel_id=1, source_target_pairs={{0,2},{2,4},{4,6},{6,8},{8,10},{10,12},{12,14},{14,16},{16,18},{18... | collective-permute-start | bytes 1544 | tf_op jit(solution)/shard_map/ppermute | solution.py:20
  1.2 12.8 %collective-permute-start.5 = (s32[128]{0:T(128)}, s32[128]{0:T(128)S(1)}, u32[]{:S(2)}, u32[]{:S(2)}) collective-permute-start(s32[128]{0:T(128)} %bitcast.377), channel_id=1, source_target_pairs={{0,30},{2,0},{4,2},{6,4},{8,6},{10,8},{12,10},{14,12},{16,14},{18,... | collective-permute-start | bytes 1544 | tf_op jit(solution)/shard_map/ppermute | solution.py:20
  7.0 16.5 %collective-permute-start = (f32[3,512]{1,0:T(4,128)S(1)}, f32[3,512]{1,0:T(4,128)S(1)}, u32[]{:S(2)}, u32[]{:S(2)}) collective-permute-start(f32[3,512]{1,0:T(4,128)S(1)} %get-tuple-element.108), channel_id=1, source_target_pairs={{0,2},{2,4},{4,6},{6,8},{8,10},{10,12},{12,14},{14,16},{16,18},{18... | collective-permute-start | bytes 18440 | tf_op jit(solution)/shard_map/ppermute | solution.py:20
  7.0 16.4 %collective-permute-start.1 = (f32[3,512]{1,0:T(4,128)S(1)}, f32[3,512]{1,0:T(4,128)S(1)}, u32[]{:S(2)}, u32[]{:S(2)}) collective-permute-start(f32[3,512]{1,0:T(4,128)S(1)} %get-tuple-element.108), channel_id=1, source_target_pairs={{0,30},{2,0},{4,2},{6,4},{8,6},{10,8},{12,10},{14,12},{16,14},{18,... | collective-permute-start | bytes 18440 | tf_op jit(solution)/shard_map/ppermute | solution.py:20
  14.1 6.7 collective-permute-start.7
  15.4 6.3 collective-permute-start.6
  23.5 208.8 %collective-permute-start.8 = (f32[3,128,256]{2,1,0:T(8,128)}, f32[3,128,256]{2,1,0:T(8,128)}, u32[]{:S(2)}, u32[]{:S(2)}) collective-permute-start(f32[3,128,256]{2,1,0:T(8,128)} %pad_maximum_fusion.3), channel_id=1, source_target_pairs={{0,30},{2,0},{4,2},{6,4},{8,6},{10,8},{12,10},{14,12},{16,14},{18,... | collective-permute-start | bytes 1179656 | tf_op jit(solution)/shard_map/ppermute | solution.py:20
  23.5 7.5 collective-permute-start.2
  27.2 5.7 collective-permute-start.3
  29.3 202.9 %collective-permute-start.9 = (f32[3,128,256]{2,1,0:T(8,128)}, f32[3,128,256]{2,1,0:T(8,128)}, u32[]{:S(2)}, u32[]{:S(2)}) collective-permute-start(f32[3,128,256]{2,1,0:T(8,128)} %pad_maximum_fusion.4), channel_id=1, source_target_pairs={{0,2},{2,4},{4,6},{6,8},{8,10},{10,12},{12,14},{14,16},{16,18},{18... | collective-permute-start | bytes 1179656 | tf_op jit(solution)/shard_map/ppermute | solution.py:20
  171.0 54.7 %copy-start.3 = (f32[640,640]{1,0:T(8,128)S(1)}, f32[640,640]{1,0:T(8,128)}, u32[]{:S(2)}) copy-start(f32[640,640]{1,0:T(8,128)} %fusion.25) | copy-start | bytes 4915204
  233.5 11.1 %collective-permute-start.10 = (f32[128,256]{1,0:T(8,128)S(1)}, f32[128,256]{1,0:T(8,128)S(1)}, u32[]{:S(2)}, u32[]{:S(2)}) collective-permute-start(f32[128,256]{1,0:T(8,128)S(1)} %get-tuple-element.58), channel_id=1, source_target_pairs={{1,0},{3,2},{5,4},{7,6},{9,8},{11,10},{13,12},{15,14},{17,16},{19,... | collective-permute-start | bytes 393224 | tf_op jit(solution)/shard_map/ppermute | solution.py:26
  234.8 9.8 %collective-permute-start.11 = (f32[128,256]{1,0:T(8,128)S(1)}, f32[128,256]{1,0:T(8,128)S(1)}, u32[]{:S(2)}, u32[]{:S(2)}) collective-permute-start(f32[128,256]{1,0:T(8,128)S(1)} %get-tuple-element.59), channel_id=1, source_target_pairs={{0,1},{2,3},{4,5},{6,7},{8,9},{10,11},{12,13},{14,15},{16,17},{18,... | collective-permute-start | bytes 393224 | tf_op jit(solution)/shard_map/ppermute | solution.py:26
  246.4 7.1 collective-permute-start.12
  246.4 7.1 collective-permute-start.13
  253.5 6.9 collective-permute-start.14
  255.2 9.7 %collective-permute-start.15 = (f32[3,128,256]{2,1,0:T(8,128)S(1)}, f32[3,128,256]{2,1,0:T(8,128)S(1)}, u32[]{:S(2)}, u32[]{:S(2)}) collective-permute-start(f32[3,128,256]{2,1,0:T(8,128)S(1)} %pad_maximum_fusion.5), channel_id=1, source_target_pairs={{1,0},{3,2},{5,4},{7,6},{9,8},{11,10},{13,12},{15,14},{17,16},{19,... | collective-permute-start | bytes 1179656 | tf_op jit(solution)/shard_map/ppermute | solution.py:26
  265.5 11.5 %collective-permute-start.16 = (f32[512,256]{1,0:T(8,128)S(1)}, f32[512,256]{1,0:T(8,128)S(1)}, u32[]{:S(2)}, u32[]{:S(2)}) collective-permute-start(f32[512,256]{1,0:T(8,128)S(1)} %convolution_add_fusion.5), channel_id=1, source_target_pairs={{0,2},{2,4},{4,6},{6,8},{8,10},{10,12},{12,14},{14,16},{16,18},{18... | collective-permute-start | bytes 1572872 | tf_op jit(solution)/shard_map/ppermute | solution.py:20
  265.5 11.4 %collective-permute-start.17 = (f32[512,256]{1,0:T(8,128)S(1)}, f32[512,256]{1,0:T(8,128)S(1)}, u32[]{:S(2)}, u32[]{:S(2)}) collective-permute-start(f32[512,256]{1,0:T(8,128)S(1)} %convolution_add_fusion.5), channel_id=1, source_target_pairs={{0,30},{2,0},{4,2},{6,4},{8,6},{10,8},{12,10},{14,12},{16,14},{18,... | collective-permute-start | bytes 1572872 | tf_op jit(solution)/shard_map/ppermute | solution.py:20
  277.1 35.5 %collective-permute-start.18 = (f32[3,512,256]{2,1,0:T(8,128)S(1)}, f32[3,512,256]{2,1,0:T(8,128)S(1)}, u32[]{:S(2)}, u32[]{:S(2)}) collective-permute-start(f32[3,512,256]{2,1,0:T(8,128)S(1)} %pad_maximum_fusion), channel_id=1, source_target_pairs={{0,1},{2,3},{4,5},{6,7},{8,9},{10,11},{12,13},{14,15},{16,17},{18,... | collective-permute-start | bytes 4718600 | tf_op jit(solution)/shard_map/ppermute | solution.py:26
  278.7 39.5 %collective-permute-start.19 = (f32[3,512,256]{2,1,0:T(8,128)S(1)}, f32[3,512,256]{2,1,0:T(8,128)S(1)}, u32[]{:S(2)}, u32[]{:S(2)}) collective-permute-start(f32[3,512,256]{2,1,0:T(8,128)S(1)} %pad_maximum_fusion), channel_id=1, source_target_pairs={{1,0},{3,2},{5,4},{7,6},{9,8},{11,10},{13,12},{15,14},{17,16},{19,... | collective-permute-start | bytes 4718600 | tf_op jit(solution)/shard_map/ppermute | solution.py:26
  434.4 6.5 collective-permute-start.20
  435.6 10.1 %collective-permute-start.21 = (f32[3,128,256]{2,1,0:T(8,128)S(1)}, f32[3,128,256]{2,1,0:T(8,128)S(1)}, u32[]{:S(2)}, u32[]{:S(2)}) collective-permute-start(f32[3,128,256]{2,1,0:T(8,128)S(1)} %pad_maximum_fusion.7), channel_id=1, source_target_pairs={{0,2},{2,4},{4,6},{6,8},{8,10},{10,12},{12,14},{14,16},{16,18},{18... | collective-permute-start | bytes 1179656 | tf_op jit(solution)/shard_map/ppermute | solution.py:20
  445.8 8.1 collective-permute-start.22
  447.1 8.0 collective-permute-start.23
  456.8 7.2 collective-permute-start.24
  456.9 7.2 collective-permute-start.25
  464.1 13.2 %collective-permute-start.26 = (f32[3,128,256]{2,1,0:T(8,128)S(1)}, f32[3,128,256]{2,1,0:T(8,128)S(1)}, u32[]{:S(2)}, u32[]{:S(2)}) collective-permute-start(f32[3,128,256]{2,1,0:T(8,128)S(1)} %pad_maximum_fusion.8), channel_id=1, source_target_pairs={{0,1},{2,3},{4,5},{6,7},{8,9},{10,11},{12,13},{14,15},{16,17},{18,... | collective-permute-start | bytes 1179656 | tf_op jit(solution)/shard_map/ppermute | solution.py:26
  468.5 12.9 %collective-permute-start.27 = (f32[3,128,256]{2,1,0:T(8,128)S(1)}, f32[3,128,256]{2,1,0:T(8,128)S(1)}, u32[]{:S(2)}, u32[]{:S(2)}) collective-permute-start(f32[3,128,256]{2,1,0:T(8,128)S(1)} %pad_maximum_fusion.8), channel_id=1, source_target_pairs={{1,0},{3,2},{5,4},{7,6},{9,8},{11,10},{13,12},{15,14},{17,16},{19,... | collective-permute-start | bytes 1179656 | tf_op jit(solution)/shard_map/ppermute | solution.py:26
  547.6 56.7 %copy-start.1 = (f32[512,256]{1,0:T(8,128)}, f32[512,256]{1,0:T(8,128)S(1)}, u32[]{:S(2)}) copy-start(f32[512,256]{1,0:T(8,128)S(1)} %multiply_add_fusion.1) | copy-start | bytes 1572868
  547.6 11.5 %collective-permute-start.28 = (f32[512,256]{1,0:T(8,128)S(1)}, f32[512,256]{1,0:T(8,128)S(1)}, u32[]{:S(2)}, u32[]{:S(2)}) collective-permute-start(f32[512,256]{1,0:T(8,128)S(1)} %multiply_add_fusion.1), channel_id=1, source_target_pairs={{0,2},{2,4},{4,6},{6,8},{8,10},{10,12},{12,14},{14,16},{16,18},{18... | collective-permute-start | bytes 1572872 | tf_op jit(solution)/shard_map/ppermute | solution.py:20
  547.7 11.4 %collective-permute-start.29 = (f32[512,256]{1,0:T(8,128)S(1)}, f32[512,256]{1,0:T(8,128)S(1)}, u32[]{:S(2)}, u32[]{:S(2)}) collective-permute-start(f32[512,256]{1,0:T(8,128)S(1)} %multiply_add_fusion.1), channel_id=1, source_target_pairs={{0,30},{2,0},{4,2},{6,4},{8,6},{10,8},{12,10},{14,12},{16,14},{18,... | collective-permute-start | bytes 1572872 | tf_op jit(solution)/shard_map/ppermute | solution.py:20
  559.2 35.6 %collective-permute-start.30 = (f32[3,512,256]{2,1,0:T(8,128)S(1)}, f32[3,512,256]{2,1,0:T(8,128)S(1)}, u32[]{:S(2)}, u32[]{:S(2)}) collective-permute-start(f32[3,512,256]{2,1,0:T(8,128)S(1)} %pad_maximum_fusion.1), channel_id=1, source_target_pairs={{0,1},{2,3},{4,5},{6,7},{8,9},{10,11},{12,13},{14,15},{16,17},{18,... | collective-permute-start | bytes 4718600 | tf_op jit(solution)/shard_map/ppermute | solution.py:26
  563.3 37.1 %collective-permute-start.31 = (f32[3,512,256]{2,1,0:T(8,128)S(1)}, f32[3,512,256]{2,1,0:T(8,128)S(1)}, u32[]{:S(2)}, u32[]{:S(2)}) collective-permute-start(f32[3,512,256]{2,1,0:T(8,128)S(1)} %pad_maximum_fusion.1), channel_id=1, source_target_pairs={{1,0},{3,2},{5,4},{7,6},{9,8},{11,10},{13,12},{15,14},{17,16},{19,... | collective-permute-start | bytes 4718600 | tf_op jit(solution)/shard_map/ppermute | solution.py:26
  648.2 8.5 collective-permute-start.32
  651.4 10.0 %collective-permute-start.33 = (f32[3,128,256]{2,1,0:T(8,128)S(1)}, f32[3,128,256]{2,1,0:T(8,128)S(1)}, u32[]{:S(2)}, u32[]{:S(2)}) collective-permute-start(f32[3,128,256]{2,1,0:T(8,128)S(1)} %pad_maximum_fusion.10), channel_id=1, source_target_pairs={{0,2},{2,4},{4,6},{6,8},{8,10},{10,12},{12,14},{14,16},{16,18},{18... | collective-permute-start | bytes 1179656 | tf_op jit(solution)/shard_map/ppermute | solution.py:20
  661.5 6.9 collective-permute-start.34
  662.8 7.1 collective-permute-start.35
  671.6 7.1 collective-permute-start.36
  671.7 7.1 collective-permute-start.37
  678.8 11.0 %collective-permute-start.38 = (f32[3,128,256]{2,1,0:T(8,128)S(1)}, f32[3,128,256]{2,1,0:T(8,128)S(1)}, u32[]{:S(2)}, u32[]{:S(2)}) collective-permute-start(f32[3,128,256]{2,1,0:T(8,128)S(1)} %pad_maximum_fusion.11), channel_id=1, source_target_pairs={{0,1},{2,3},{4,5},{6,7},{8,9},{10,11},{12,13},{14,15},{16,17},{18,... | collective-permute-start | bytes 1179656 | tf_op jit(solution)/shard_map/ppermute | solution.py:26
  683.2 10.7 %collective-permute-start.39 = (f32[3,128,256]{2,1,0:T(8,128)S(1)}, f32[3,128,256]{2,1,0:T(8,128)S(1)}, u32[]{:S(2)}, u32[]{:S(2)}) collective-permute-start(f32[3,128,256]{2,1,0:T(8,128)S(1)} %pad_maximum_fusion.11), channel_id=1, source_target_pairs={{1,0},{3,2},{5,4},{7,6},{9,8},{11,10},{13,12},{15,14},{17,16},{19,... | collective-permute-start | bytes 1179656 | tf_op jit(solution)/shard_map/ppermute | solution.py:26
  690.4 69.5 %copy-start.2 = (f32[512,256]{1,0:T(8,128)S(1)}, f32[512,256]{1,0:T(8,128)}, u32[]{:S(2)}) copy-start(f32[512,256]{1,0:T(8,128)} %copy-done.1) | copy-start | bytes 1572868
  760.0 11.5 %collective-permute-start.40 = (f32[512,256]{1,0:T(8,128)S(1)}, f32[512,256]{1,0:T(8,128)S(1)}, u32[]{:S(2)}, u32[]{:S(2)}) collective-permute-start(f32[512,256]{1,0:T(8,128)S(1)} %multiply_add_fusion), channel_id=1, source_target_pairs={{0,2},{2,4},{4,6},{6,8},{8,10},{10,12},{12,14},{14,16},{16,18},{18... | collective-permute-start | bytes 1572872 | tf_op jit(solution)/shard_map/ppermute | solution.py:20
  760.1 11.4 %collective-permute-start.41 = (f32[512,256]{1,0:T(8,128)S(1)}, f32[512,256]{1,0:T(8,128)S(1)}, u32[]{:S(2)}, u32[]{:S(2)}) collective-permute-start(f32[512,256]{1,0:T(8,128)S(1)} %multiply_add_fusion), channel_id=1, source_target_pairs={{0,30},{2,0},{4,2},{6,4},{8,6},{10,8},{12,10},{14,12},{16,14},{18,... | collective-permute-start | bytes 1572872 | tf_op jit(solution)/shard_map/ppermute | solution.py:20
  771.6 35.4 %collective-permute-start.42 = (f32[3,512,256]{2,1,0:T(8,128)S(1)}, f32[3,512,256]{2,1,0:T(8,128)S(1)}, u32[]{:S(2)}, u32[]{:S(2)}) collective-permute-start(f32[3,512,256]{2,1,0:T(8,128)S(1)} %pad_maximum_fusion.2), channel_id=1, source_target_pairs={{0,1},{2,3},{4,5},{6,7},{8,9},{10,11},{12,13},{14,15},{16,17},{18,... | collective-permute-start | bytes 4718600 | tf_op jit(solution)/shard_map/ppermute | solution.py:26
  774.0 38.5 %collective-permute-start.43 = (f32[3,512,256]{2,1,0:T(8,128)S(1)}, f32[3,512,256]{2,1,0:T(8,128)S(1)}, u32[]{:S(2)}, u32[]{:S(2)}) collective-permute-start(f32[3,512,256]{2,1,0:T(8,128)S(1)} %pad_maximum_fusion.2), channel_id=1, source_target_pairs={{1,0},{3,2},{5,4},{7,6},{9,8},{11,10},{13,12},{15,14},{17,16},{19,... | collective-permute-start | bytes 4718600 | tf_op jit(solution)/shard_map/ppermute | solution.py:26
  (5 other events, 28.5 us)
